TPU v7x, 256 devices: a whole 4x4x8 slice. The times are simulated.
256 devices in a mesh: gx: 32 (over z, x), gy: 8 (over y, core).
Axes of the slice: x: 4, y: 4, z: 8, core: 2. Of those that a mesh axis runs over, the one named last changes fastest.
Arguments:
- velocity: float32 [2, 2048, 4096], P(None, 'gy', 'gx'), may hold values from -3 to 3
- stress: float32 [3, 2048, 4096], P(None, 'gy', 'gx'), may hold values from -3 to 3
- ice_mass: float32 [2048, 4096], P('gy', 'gx'), may hold values from 0.5 to 4
- strength: float32 [2048, 4096], P('gy', 'gx'), may hold values from 0.2 to 2
- land_mask: int32 [2048, 4096], P('gy', 'gx'), may hold values from 0 to 1
- ocean_forcing: float32 [4, 2048, 4096], P(None, ('gy', 'gx')), may hold values from -3 to 3
Outputs:
- velocity_out: float32 [2, 2048, 4096], P(None, 'gy', 'gx')
- stress_out: float32 [3, 2048, 4096], P(None, 'gy', 'gx')
- residuals: float32 [4], replicated
- ocean_stress: float32 [2, 2048, 4096], P(None, ('gy', 'gx'))
All inputs are finite; a program needn't handle non-finite values.
Results may differ from a plain program's by a relative error of at most 0.0001.
Values sent between devices are 32-bit elements; how exact they have to be, the bound alone decides.
A program may use at most 64 MiB of HBM per device.

v0:
```python
import jax
import jax.numpy as jnp
from jax import lax
from jax.sharding import Mesh
from jax.sharding import PartitionSpec as P

ITERS = 4
GX = ("gx_0", "gx_1")
GY = ("gy_0", "gy_1")
GX_GY = ("gx_0", "gx_1", "gy_0", "gy_1")
GY_GX = ("gy_0", "gy_1", "gx_0", "gx_1")
ALPHA = 4.0
BETA = 4.0
WATER_DRAG = 1.0
DELTA_FLOOR = 0.0025


def cut_along(array, dim, count):
    before, after = (array.shape[:dim], array.shape[dim + 1 :])
    return jnp.moveaxis(array.reshape(*before, count, -1, *after), dim, 0)


def joined_along(parts, dim):
    lengths = list(parts.shape[1:])
    lengths[dim] *= parts.shape[0]
    return jnp.moveaxis(parts, 0, dim).reshape(lengths)


def moved_by_axis(parts, axes, order):
    inside = parts.shape[1:]
    filled = parts.reshape(*(lax.axis_size(a) for a in axes), *inside)
    for k in order:
        filled = lax.all_to_all(filled, axes[k], k, k, tiled=True)
    return filled.reshape(-1, *inside)


def one_axis_at_a_time(array, axes, order, split_dim, concat_dim):
    parts = cut_along(array, split_dim, lax.axis_size(axes))
    return joined_along(moved_by_axis(parts, axes, order), concat_dim)


def extended(cells, sides, width):
    for axis, dim in sides:
        count = lax.axis_size(axis)
        head = lax.slice_in_dim(cells, 0, width, axis=dim)
        tail = lax.slice_in_dim(cells, cells.shape[dim] - width, cells.shape[dim], axis=dim)
        cells = jnp.concatenate(
            [
                lax.ppermute(tail, axis, [(i, (i + 1) % count) for i in range(count)]),
                cells,
                lax.ppermute(head, axis, [((i + 1) % count, i) for i in range(count)]),
            ],
            axis=dim,
        )
    return cells


def over_axes(array, axes):
    for axis in axes:
        array = lax.psum(array, axis)
    return array


def diff_east(padded):
    return 0.5 * (padded[..., 1:-1, 2:] - padded[..., 1:-1, :-2])


def diff_north(padded):
    return 0.5 * (padded[..., 2:, 1:-1] - padded[..., :-2, 1:-1])


def trim_edges(field, level):
    if level == 0:
        return field
    return field[..., level:-level, level:-level]


def record_sum(own_sum, local_sums):
    local_sums.append(own_sum)


def relax_stress(padded_vel, stress, strength, ice_frac):
    east_dx = diff_east(padded_vel[0])
    east_dy = diff_north(padded_vel[0])
    north_dx = diff_east(padded_vel[1])
    north_dy = diff_north(padded_vel[1])
    divergence = east_dx + north_dy
    tension = east_dx - north_dy
    shear_rate = east_dy + north_dx
    delta_rate = jnp.sqrt(
        divergence * divergence + 0.25 * (tension * tension + shear_rate * shear_rate) + DELTA_FLOOR
    )
    target = jnp.stack(
        [
            strength * (divergence / delta_rate - 1.0),
            strength * tension / (4.0 * delta_rate),
            strength * shear_rate / (8.0 * delta_rate),
        ]
    )
    return (stress + (target - stress) / ALPHA) * ice_frac


def drag_coeff(vel, currents):
    east_gap = currents[0] - vel[0]
    north_gap = currents[1] - vel[1]
    return WATER_DRAG * jnp.sqrt(east_gap * east_gap + north_gap * north_gap + 0.01)


def relax_velocity(padded_stress, vel, vel_start, forcing, ice_mass, coriolis, ice_frac):
    normal_xx = 0.5 * (padded_stress[0] + padded_stress[1])
    normal_yy = 0.5 * (padded_stress[0] - padded_stress[1])
    shear_xy = padded_stress[2]
    force_east = diff_east(normal_xx) + diff_north(shear_xy)
    force_north = diff_east(shear_xy) + diff_north(normal_yy)
    drag_rate = drag_coeff(vel, forcing[2:4])
    denominator = BETA + 1.0 + drag_rate / ice_mass
    new_east = (
        (
            BETA * vel[0]
            + vel_start[0]
            + (force_east + forcing[0] + drag_rate * forcing[2]) / ice_mass
            + coriolis * vel[1]
        )
        / denominator
        * ice_frac
    )
    new_north = (
        (
            BETA * vel[1]
            + vel_start[1]
            + (force_north + forcing[1] + drag_rate * forcing[3]) / ice_mass
            - coriolis * vel[0]
        )
        / denominator
        * ice_frac
    )
    return jnp.stack([new_east, new_north])


def local(velocity, stress, ice_mass, strength, land_mask, ocean_forcing):
    row_count = velocity.shape[1]
    col_count = velocity.shape[2]
    forcing = one_axis_at_a_time(ocean_forcing, GX, (0, 1), 2, 1)
    ice_frac = land_mask.astype(jnp.float32)
    lat_band = lax.axis_index(GY)
    total_rows = lax.axis_size(GY) * row_count
    local_sums = []
    depth = 2 * ITERS
    stacked = jnp.concatenate(
        [velocity, stress, strength[None], ice_mass[None], ice_frac[None], forcing], axis=0
    )
    padded = extended(stacked, ((GX, 2), (GY, 1)), depth)
    wide_rows = lat_band * row_count - depth + jnp.arange(row_count + 2 * depth, dtype=jnp.int32)
    inside = ((wide_rows >= 0) & (wide_rows < total_rows)).astype(jnp.float32)[:, None]
    wide_vel = padded[0:2] * inside
    wide_stress = padded[2:5] * inside
    wide_strength = padded[5]
    wide_mass = padded[6]
    wide_ice = padded[7] * inside
    wide_forcing = padded[8:12]
    wide_lat = wide_rows.astype(jnp.float32)
    wide_coriolis = jnp.broadcast_to(
        (0.3 + 1.2 * (wide_lat + 0.5) / total_rows)[:, None],
        (row_count + 2 * depth, col_count + 2 * depth),
    )
    vel_work = wide_vel
    stress_work = wide_stress
    margin = depth
    for subcycle in range(ITERS):
        level_one = depth - (margin - 1)
        stress_cut = (stress_work.shape[-1] - (col_count + 2 * (margin - 1))) // 2
        stress_work = relax_stress(
            vel_work,
            trim_edges(stress_work, stress_cut),
            trim_edges(wide_strength, level_one),
            trim_edges(wide_ice, level_one),
        )
        level_two = depth - (margin - 2)
        old_vel = trim_edges(vel_work, 2)
        new_vel = relax_velocity(
            stress_work,
            old_vel,
            trim_edges(wide_vel, level_two),
            trim_edges(wide_forcing, level_two),
            trim_edges(wide_mass, level_two),
            trim_edges(wide_coriolis, level_two),
            trim_edges(wide_ice, level_two),
        )
        change = trim_edges(new_vel - old_vel, margin - 2)
        record_sum(jnp.sum(change * change), local_sums)
        vel_work = new_vel
        margin = margin - 2
    stress = trim_edges(stress_work, 1)
    history = over_axes(jnp.stack(local_sums), GX_GY)
    drag_rate = drag_coeff(vel_work, forcing[2:4])
    ice_stress = drag_rate * (vel_work - forcing[2:4]) * ice_frac
    ocean_stress = lax.all_to_all(ice_stress, GX, split_axis=1, concat_axis=2, tiled=True)
    return (vel_work, stress, history, ocean_stress)


def solution(mesh):
    torus = Mesh(mesh.devices.reshape(8, 4, 4, 2), ("gx_0", "gx_1", "gy_0", "gy_1"))
    placed = (
        P(None, GY, GX),
        P(None, GY, GX),
        P(GY, GX),
        P(GY, GX),
        P(GY, GX),
        P(None, GY_GX, None),
    )
    return jax.shard_map(
        local,
        mesh=torus,
        in_specs=placed,
        out_specs=(P(None, GY, GX), P(None, GY, GX), P(), P(None, GY_GX, None)),
        check_vma=False,
    )
```

profile of v0, /device:TPU:1, one launch (start us, length us, event | category | flops | bytes accessed | tf_op | source)
XLA Modules:
  0.0 139.0 jit_solution(16432302177492272811)
XLA Ops:
  0.6 1.2 copy.50
  1.8 1.1 copy.32
  3.0 9.1 %all-to-all-start = ((f32[8,4,4,8,128]{4,3,1,2,0:T(8,128)}), f32[8,4,4,8,128]{4,3,1,2,0:T(8,128)S(1)}, u32[]{:S(2)}, u32[]{:S(2)}) async-start(f32[8,4,4,8,128]{4,3,1,2,0:T(8,128)} %copy.32), calls=%async_computation | async-start | bytes 1048576 | tf_op jit(solution)/shard_map/all_to_all | solution.py:33
  12.3 17.8 %all-to-all-done = f32[8,4,4,8,128]{4,3,1,2,0:T(8,128)S(1)} async-done(((f32[8,4,4,8,128]{4,3,1,2,0:T(8,128)}), f32[8,4,4,8,128]{4,3,1,2,0:T(8,128)S(1)}, u32[]{:S(2)}, u32[]{:S(2)}) %all-to-all-start) | async-done | bytes 524320 | tf_op jit(solution)/shard_map/all_to_all | solution.py:33
  30.1 0.9 copy.33
  30.9 4.0 %all-to-all-start.1 = ((f32[8,4,4,8,128]{4,3,0,2,1:T(8,128)}), f32[8,4,4,8,128]{4,3,0,2,1:T(8,128)S(1)}, u32[]{:S(2)}, u32[]{:S(2)}) async-start(f32[8,4,4,8,128]{4,3,0,2,1:T(8,128)} %copy.33), calls=%async_computation.1 | async-start | bytes 1048576 | tf_op jit(solution)/shard_map/all_to_all | solution.py:33
  35.1 8.6 %all-to-all-done.1 = f32[8,4,4,8,128]{4,3,0,2,1:T(8,128)S(1)} async-done(((f32[8,4,4,8,128]{4,3,0,2,1:T(8,128)}), f32[8,4,4,8,128]{4,3,0,2,1:T(8,128)S(1)}, u32[]{:S(2)}, u32[]{:S(2)}) %all-to-all-start.1) | async-done | bytes 524320 | tf_op jit(solution)/shard_map/all_to_all | solution.py:33
  43.8 0.8 copy-done.3
  44.6 1.7 %fusion.150 = (f32[12,256,8]{2,1,0:T(8,128)}, f32[12,256,8]{2,1,0:T(8,128)S(1)}) fusion(f32[12,256,128]{2,1,0:T(8,128)S(1)} %bitcast_dynamic-update-slice_fusion), kind=kLoop, calls=%fused_computation.281 | loop fusion | bytes 393216 | tf_op jit(solution)/shard_map/slice | solution.py:46
  46.3 1.8 %copy.36 = f32[12,256,8]{1,2,0:T(8,128)S(1)} copy(f32[12,256,8]{2,1,0:T(8,128)} %get-tuple-element.37) | data formatting | bytes 196608 | tf_op jit(solution)/shard_map/slice | solution.py:46
  48.1 0.3 collective-permute-start
  48.5 1.1 copy.37
  49.6 4.5 %collective-permute-start.1 = (f32[12,256,8]{1,2,0:T(8,128)}, f32[12,256,8]{1,2,0:T(8,128)}, u32[]{:S(2)}, u32[]{:S(2)}) collective-permute-start(f32[12,256,8]{1,2,0:T(8,128)} %copy.37), channel_id=1, source_target_pairs={{8,0},{16,8},{24,16},{32,24},{40,32},{48,40},{56,48},{64,56},{72,6... | collective-permute-start | bytes 294920 | tf_op jit(solution)/shard_map/ppermute | solution.py:51
  54.1 0.8 collective-permute-done
  55.0 0.5 copy.38
  55.5 0.6 collective-permute-done.1
  56.0 2.5 %copy.39 = f32[12,256,8]{2,1,0:T(8,128)} copy(f32[12,256,8]{1,2,0:T(8,128)} %collective-permute-done.1) | data formatting | bytes 196608 | tf_op jit(solution)/shard_map/ppermute | solution.py:51
  58.5 1.1 pad_maximum_fusion.7
  59.6 4.0 %collective-permute-start.2 = (f32[12,8,144]{2,1,0:T(8,128)S(1)}, f32[12,8,144]{2,1,0:T(8,128)S(1)}, u32[]{:S(2)}, u32[]{:S(2)}) collective-permute-start(f32[12,8,144]{2,1,0:T(8,128)S(1)} %get-tuple-element.33), channel_id=1, source_target_pairs={{0,1},{1,2},{2,3},{3,4},{4,5},{5,6},{6,7},{7,0},{8,9},{9,10},{10,1... | collective-permute-start | bytes 165896 | tf_op jit(solution)/shard_map/ppermute | solution.py:49
  63.7 1.5 %collective-permute-done.2 = f32[12,8,144]{2,1,0:T(8,128)S(1)} collective-permute-done((f32[12,8,144]{2,1,0:T(8,128)S(1)}, f32[12,8,144]{2,1,0:T(8,128)S(1)}, u32[]{:S(2)}, u32[]{:S(2)}) %collective-permute-start.2) | collective-permute-done | bytes 55328 | tf_op jit(solution)/shard_map/ppermute | solution.py:49
  65.2 2.4 %collective-permute-done.3 = f32[12,8,144]{2,1,0:T(8,128)S(1)} collective-permute-done((f32[12,8,144]{2,1,0:T(8,128)S(1)}, f32[12,8,144]{2,1,0:T(8,128)S(1)}, u32[]{:S(2)}, u32[]{:S(2)}) %collective-permute-start.3) | collective-permute-done | bytes 55328 | tf_op jit(solution)/shard_map/ppermute | solution.py:51
  67.6 1.3 pad_maximum_fusion
  69.7 0.9 copy-done
  70.7 0.6 multiply_bitcast_fusion.5
  71.6 0.9 slice-done
  72.5 0.3 fusion.2
  72.9 1.5 %copy-done.1 = f32[12,272,144]{2,1,0:T(8,128)S(1)} copy-done((f32[12,272,144]{2,1,0:T(8,128)S(1)}, f32[12,272,144]{2,1,0:T(8,128)}, u32[]{:S(2)}) %copy-start.1) | copy-done | bytes 1880088
  74.4 0.9 fusion.15
  75.3 0.9 fusion.19
  76.2 0.6 multiply_bitcast_fusion.2
  77.4 0.9 fusion.83
  78.4 0.9 fusion.71
  79.3 0.6 multiply_bitcast_fusion.11
  80.5 0.9 fusion.59
  81.5 1.1 fusion.48
  82.6 0.6 multiply_bitcast_fusion.8
  83.8 0.7 copy-done.4
  84.5 0.5 add_sqrt_fusion.7
  85.1 0.9 copy.41
  86.0 7.1 %all-to-all-start.2 = ((f32[2,256,128]{2,0,1:T(2,128)}), f32[2,256,128]{2,0,1:T(2,128)S(1)}, u32[]{:S(2)}, u32[]{:S(2)}) async-start(f32[2,256,128]{2,0,1:T(2,128)} %copy.41), calls=%async_computation.2 | async-start | bytes 524288 | tf_op jit(solution)/shard_map/all_to_all | solution.py:197
  93.3 1.2 fusion.98
  94.6 2.7 %pad_maximum_fusion.8 = f32[4]{0:T(128)S(1)} fusion(f32[1]{0:T(128)} %bitcast.80, f32[1]{0:T(128)} %bitcast.79, f32[1]{0:T(128)} %bitcast.78, f32[1]{0:T(128)} %bitcast.77), kind=kLoop, calls=%fused_computation.280 | loop fusion | flops 12 | bytes 32 | tf_op jit(solution)/shard_map/stack | solution.py:194
  97.3 13.8 %psum.28 = f32[4]{0:T(128)S(1)} all-reduce(f32[4]{0:T(128)S(1)} %pad_maximum_fusion.8), channel_id=1, replica_groups=mesh['gx_0'=8,'gx_1'=4,'gy_0'=4,'gy_1'=2] {'gx_0'}, use_global_device_ids=true, to_apply=%region_4.0 | all-reduce | flops 4 | bytes 32 | tf_op jit(solution)/shard_map/psum | solution.py:60
  111.0 8.4 %psum.29 = f32[4]{0:T(128)S(1)} all-reduce(f32[4]{0:T(128)S(1)} %psum.28), channel_id=1, replica_groups=mesh['gx_0'=8,'gx_1'=4,'gy_0'=4,'gy_1'=2] {'gx_1'}, use_global_device_ids=true, to_apply=%region_5.0 | all-reduce | flops 4 | bytes 32 | tf_op jit(solution)/shard_map/psum | solution.py:60
  119.4 8.3 %psum.30 = f32[4]{0:T(128)S(1)} all-reduce(f32[4]{0:T(128)S(1)} %psum.29), channel_id=1, replica_groups=mesh['gx_0'=8,'gx_1'=4,'gy_0'=4,'gy_1'=2] {'gy_0'}, use_global_device_ids=true, to_apply=%region_6.0 | all-reduce | flops 4 | bytes 32 | tf_op jit(solution)/shard_map/psum | solution.py:60
  127.7 9.7 %psum.31 = f32[4]{0:T(128)} all-reduce(f32[4]{0:T(128)S(1)} %psum.30), channel_id=1, replica_groups=mesh['gx_0'=8,'gx_1'=4,'gy_0'=4,'gy_1'=2] {'gy_1'}, use_global_device_ids=true, to_apply=%region_7.0 | all-reduce | flops 4 | bytes 32 | tf_op jit(solution)/shard_map/psum | solution.py:60
  137.3 0.9 slice.886
  138.3 0.7 copy.51
  (56 shorter events, 3.9 us)
Async XLA Ops:
  0.6 11.5 %copy-start.8 = (f32[2,256,128]{2,1,0:T(8,128)S(1)}, f32[2,256,128]{2,1,0:T(8,128)}, u32[]{:S(2)}) copy-start(f32[2,256,128]{2,1,0:T(8,128)} %param.6) | copy-start | bytes 786436
  1.8 10.3 %copy-start.7 = (f32[3,256,128]{2,1,0:T(8,128)S(1)}, f32[3,256,128]{2,1,0:T(8,128)}, u32[]{:S(2)}) copy-start(f32[3,256,128]{2,1,0:T(8,128)} %param.7) | copy-start | bytes 1179652
  1.8 10.4 %copy-start.9 = (f32[256,128]{1,0:T(8,128)S(1)}, f32[256,128]{1,0:T(8,128)}, u32[]{:S(2)}) copy-start(f32[256,128]{1,0:T(8,128)} %param.9) | copy-start | bytes 393220
  3.0 9.3 %copy-start.10 = (f32[256,128]{1,0:T(8,128)S(1)}, f32[256,128]{1,0:T(8,128)}, u32[]{:S(2)}) copy-start(f32[256,128]{1,0:T(8,128)} %param.8) | copy-start | bytes 393220
  3.0 27.1 %all-to-all-start = ((f32[8,4,4,8,128]{4,3,1,2,0:T(8,128)}), f32[8,4,4,8,128]{4,3,1,2,0:T(8,128)S(1)}, u32[]{:S(2)}, u32[]{:S(2)}) async-start(f32[8,4,4,8,128]{4,3,1,2,0:T(8,128)} %copy.32), calls=%async_computation | async-start | bytes 1048576 | tf_op jit(solution)/shard_map/all_to_all | solution.py:33
  12.2 23.0 %copy-start.6 = (s32[256,128]{1,0:T(8,128)S(1)}, s32[256,128]{1,0:T(8,128)}, u32[]{:S(2)}) copy-start(s32[256,128]{1,0:T(8,128)} %param.10) | copy-start | bytes 393220
  30.9 12.8 %all-to-all-start.1 = ((f32[8,4,4,8,128]{4,3,0,2,1:T(8,128)}), f32[8,4,4,8,128]{4,3,0,2,1:T(8,128)S(1)}, u32[]{:S(2)}, u32[]{:S(2)}) async-start(f32[8,4,4,8,128]{4,3,0,2,1:T(8,128)} %copy.33), calls=%async_computation.1 | async-start | bytes 1048576 | tf_op jit(solution)/shard_map/all_to_all | solution.py:33
  43.8 0.8 copy-start.3
  48.1 6.8 %collective-permute-start = (f32[12,256,8]{1,2,0:T(8,128)S(1)}, f32[12,256,8]{1,2,0:T(8,128)S(1)}, u32[]{:S(2)}, u32[]{:S(2)}) collective-permute-start(f32[12,256,8]{1,2,0:T(8,128)S(1)} %copy.36), channel_id=1, source_target_pairs={{0,8},{8,16},{16,24},{24,32},{32,40},{40,48},{48,56},{56,64},{64,7... | collective-permute-start | bytes 294920 | tf_op jit(solution)/shard_map/ppermute | solution.py:49
  49.6 6.5 %collective-permute-start.1 = (f32[12,256,8]{1,2,0:T(8,128)}, f32[12,256,8]{1,2,0:T(8,128)}, u32[]{:S(2)}, u32[]{:S(2)}) collective-permute-start(f32[12,256,8]{1,2,0:T(8,128)} %copy.37), channel_id=1, source_target_pairs={{8,0},{16,8},{24,16},{32,24},{40,32},{48,40},{56,48},{64,56},{72,6... | collective-permute-start | bytes 294920 | tf_op jit(solution)/shard_map/ppermute | solution.py:51
  58.5 9.1 %copy-start.2 = (f32[12,256,8]{2,1,0:T(8,128)S(1)}, f32[12,256,8]{2,1,0:T(8,128)}, u32[]{:S(2)}) copy-start(f32[12,256,8]{2,1,0:T(8,128)} %copy.39) | copy-start | bytes 294916
  59.6 5.6 %collective-permute-start.2 = (f32[12,8,144]{2,1,0:T(8,128)S(1)}, f32[12,8,144]{2,1,0:T(8,128)S(1)}, u32[]{:S(2)}, u32[]{:S(2)}) collective-permute-start(f32[12,8,144]{2,1,0:T(8,128)S(1)} %get-tuple-element.33), channel_id=1, source_target_pairs={{0,1},{1,2},{2,3},{3,4},{4,5},{5,6},{6,7},{7,0},{8,9},{9,10},{10,1... | collective-permute-start | bytes 165896 | tf_op jit(solution)/shard_map/ppermute | solution.py:49
  63.6 4.0 %collective-permute-start.3 = (f32[12,8,144]{2,1,0:T(8,128)S(1)}, f32[12,8,144]{2,1,0:T(8,128)S(1)}, u32[]{:S(2)}, u32[]{:S(2)}) collective-permute-start(f32[12,8,144]{2,1,0:T(8,128)S(1)} %get-tuple-element.34), channel_id=1, source_target_pairs={{1,0},{2,1},{3,2},{4,3},{5,4},{6,5},{7,6},{0,7},{9,8},{10,9},{11,1... | collective-permute-start | bytes 165896 | tf_op jit(solution)/shard_map/ppermute | solution.py:51
  68.9 1.7 %copy-start = (f32[12,272,144]{2,1,0:T(8,128)}, f32[12,272,144]{2,1,0:T(8,128)S(1)}, u32[]{:S(2)}) copy-start(f32[12,272,144]{2,1,0:T(8,128)S(1)} %pad_maximum_fusion) | copy-start | bytes 5640196
  71.3 1.2 slice-start
  72.5 1.9 %copy-start.1 = (f32[12,272,144]{2,1,0:T(8,128)S(1)}, f32[12,272,144]{2,1,0:T(8,128)}, u32[]{:S(2)}) copy-start(f32[12,272,144]{2,1,0:T(8,128)} %copy-done) | copy-start | bytes 5640196
  83.5 1.0 copy-start.4
  85.1 9.5 %copy-start.5 = (f32[2,256,128]{2,1,0:T(8,128)}, f32[2,256,128]{2,1,0:T(8,128)S(1)}, u32[]{:S(2)}) copy-start(f32[2,256,128]{2,1,0:T(8,128)S(1)} %get-tuple-element.13) | copy-start | bytes 786436
  86.0 52.2 %all-to-all-start.2 = ((f32[2,256,128]{2,0,1:T(2,128)}), f32[2,256,128]{2,0,1:T(2,128)S(1)}, u32[]{:S(2)}, u32[]{:S(2)}) async-start(f32[2,256,128]{2,0,1:T(2,128)} %copy.41), calls=%async_computation.2 | async-start | bytes 524288 | tf_op jit(solution)/shard_map/all_to_all | solution.py:197
where the time goes:
time: 140 us; the launch traced here: 139 us
  blocking collectives  40.1 us (29%)
  waiting for transfers between devices  31.7 us (23%)
  starting transfers between devices  29.1 us (21%)
  local copies, waits for them, and re-layouts  19.5 us (14%)
  other arithmetic  17.7 us (13%)
    psum x4, blocking collectives, over_axes(): array = lax.psum(array, axis)  40.1 us
    all_to_all x2, waiting for transfers between devices, moved_by_axis(): filled = lax.all_to_all(filled, axes[k], k, k, tiled=True)  26.4 us
    all_to_all x2, starting transfers between devices, moved_by_axis(): filled = lax.all_to_all(filled, axes[k], k, k, tiled=True)  13.1 us
    all_to_all x1, starting transfers between devices, local(): lax.all_to_all(ice_stress, GX, split_axis=1, concat_axis=2, tiled=True)  7.11 us
    unnamed x27, local copies, waits for them, and re-layouts  5.2 us
    ppermute x2, starting transfers between devices, extended(): lax.ppermute(head, axis, [((i + 1) % count, i) for i in range(count)])  4.5 us
    ppermute x2, starting transfers between devices, extended(): lax.ppermute(tail, axis, [(i, (i + 1) % count) for i in range(count)])  4.3 us
    slice x2, local copies, waits for them, and re-layouts, extended(): lax.slice_in_dim(cells, cells.shape[dim] - width, cells.shape[dim], axis=...  3.52 us
  transfers between devices with their start and end apart: 7, of which 6 were waited for; matrix products, arithmetic and copies ran while one was open for 5% of the time, Pallas kernels for 0%

commit v1 on v0

--- a/solution.py
+++ b/solution.py
@@ -57,7 +57,7 @@
 
 def over_axes(array, axes):
     for axis in axes:
-        array = lax.psum(array, axis)
+        array = jnp.sum(lax.all_gather(array, axis), axis=0)
     return array
 
 

time: 140 us -> 146 us (1.043)
  local copies, waits for them, and re-layouts: 19.5 us -> 22.9 us
  between operations: 1.03 us -> 3.7 us
    psum x4 -> x0, blocking collectives: 40.1 us -> none  [over_axes(): array = lax.psum(array, axis)]
    unnamed x0 -> x4, blocking collectives: none -> 39.5 us
    unnamed x27 -> x46, local copies, waits for them, and re-layouts: 5.2 us -> 8.29 us
    another operation x1 -> x0, other arithmetic: 2.67 us -> none  [local(): history = over_axes(jnp.stack(local_sums), GX_GY)]
    unnamed x1 -> x2, other arithmetic: 0.01 us -> 2.61 us
  transfers between devices with their start and end apart: 7 -> 7, of which waited for: 6 -> 6; matrix products, arithmetic and copies ran while one was open for 5% -> 8% of each run, Pallas kernels for 0% -> 0%
where the time goes in v1:
time: 146 us; the launch traced here: 145 us
  blocking collectives  39.5 us (27%)
  waiting for transfers between devices  31.7 us (22%)
  starting transfers between devices  29.1 us (20%)
  local copies, waits for them, and re-layouts  22.9 us (16%)
  other arithmetic  18.1 us (12%)
  between operations  3.7 us (3%)
    unnamed x4, blocking collectives  39.5 us
    all_to_all x2, waiting for transfers between devices, moved_by_axis(): filled = lax.all_to_all(filled, axes[k], k, k, tiled=True)  26.4 us
    all_to_all x2, starting transfers between devices, moved_by_axis(): filled = lax.all_to_all(filled, axes[k], k, k, tiled=True)  13.1 us
    unnamed x46, local copies, waits for them, and re-layouts  8.29 us
    all_to_all x1, starting transfers between devices, local(): lax.all_to_all(ice_stress, GX, split_axis=1, concat_axis=2, tiled=True)  7.11 us
    ppermute x2, starting transfers between devices, extended(): lax.ppermute(head, axis, [((i + 1) % count, i) for i in range(count)])  4.5 us
    ppermute x2, starting transfers between devices, extended(): lax.ppermute(tail, axis, [(i, (i + 1) % count) for i in range(count)])  4.3 us
    slice x2, local copies, waits for them, and re-layouts, extended(): lax.slice_in_dim(cells, cells.shape[dim] - width, cells.shape[dim], axis=...  3.52 us
  transfers between devices with their start and end apart: 7, of which 6 were waited for; matrix products, arithmetic and copies ran while one was open for 8% of the time, Pallas kernels for 0%

profile of v1, /device:TPU:1, one launch (start us, length us, event | category | flops | bytes accessed | tf_op | source)
XLA Modules:
  0.0 145.0 jit_solution(2726343755813837493)
XLA Ops:
  0.6 1.2 copy.50
  1.8 1.1 copy.32
  2.9 9.1 %all-to-all-start = ((f32[8,4,4,8,128]{4,3,1,2,0:T(8,128)}), f32[8,4,4,8,128]{4,3,1,2,0:T(8,128)S(1)}, u32[]{:S(2)}, u32[]{:S(2)}) async-start(f32[8,4,4,8,128]{4,3,1,2,0:T(8,128)} %copy.32), calls=%async_computation | async-start | bytes 1048576 | tf_op jit(solution)/shard_map/all_to_all | solution.py:33
  12.2 17.8 %all-to-all-done = f32[8,4,4,8,128]{4,3,1,2,0:T(8,128)S(1)} async-done(((f32[8,4,4,8,128]{4,3,1,2,0:T(8,128)}), f32[8,4,4,8,128]{4,3,1,2,0:T(8,128)S(1)}, u32[]{:S(2)}, u32[]{:S(2)}) %all-to-all-start) | async-done | bytes 524320 | tf_op jit(solution)/shard_map/all_to_all | solution.py:33
  30.0 0.8 copy.33
  30.9 4.0 %all-to-all-start.1 = ((f32[8,4,4,8,128]{4,3,0,2,1:T(8,128)}), f32[8,4,4,8,128]{4,3,0,2,1:T(8,128)S(1)}, u32[]{:S(2)}, u32[]{:S(2)}) async-start(f32[8,4,4,8,128]{4,3,0,2,1:T(8,128)} %copy.33), calls=%async_computation.1 | async-start | bytes 1048576 | tf_op jit(solution)/shard_map/all_to_all | solution.py:33
  35.1 8.6 %all-to-all-done.1 = f32[8,4,4,8,128]{4,3,0,2,1:T(8,128)S(1)} async-done(((f32[8,4,4,8,128]{4,3,0,2,1:T(8,128)}), f32[8,4,4,8,128]{4,3,0,2,1:T(8,128)S(1)}, u32[]{:S(2)}, u32[]{:S(2)}) %all-to-all-start.1) | async-done | bytes 524320 | tf_op jit(solution)/shard_map/all_to_all | solution.py:33
  43.8 0.8 copy-done.3
  44.6 1.7 %fusion.150 = (f32[12,256,8]{2,1,0:T(8,128)}, f32[12,256,8]{2,1,0:T(8,128)S(1)}) fusion(f32[12,256,128]{2,1,0:T(8,128)S(1)} %bitcast_dynamic-update-slice_fusion), kind=kLoop, calls=%fused_computation.281 | loop fusion | bytes 393216 | tf_op jit(solution)/shard_map/slice | solution.py:46
  46.3 1.8 %copy.36 = f32[12,256,8]{1,2,0:T(8,128)S(1)} copy(f32[12,256,8]{2,1,0:T(8,128)} %get-tuple-element.37) | data formatting | bytes 196608 | tf_op jit(solution)/shard_map/slice | solution.py:46
  48.5 1.1 copy.37
  49.6 4.5 %collective-permute-start.1 = (f32[12,256,8]{1,2,0:T(8,128)}, f32[12,256,8]{1,2,0:T(8,128)}, u32[]{:S(2)}, u32[]{:S(2)}) collective-permute-start(f32[12,256,8]{1,2,0:T(8,128)} %copy.37), channel_id=1, source_target_pairs={{8,0},{16,8},{24,16},{32,24},{40,32},{48,40},{56,48},{64,56},{72,6... | collective-permute-start | bytes 294920 | tf_op jit(solution)/shard_map/ppermute | solution.py:51
  54.1 0.8 collective-permute-done
  55.4 0.6 collective-permute-done.1
  56.0 2.5 %copy.39 = f32[12,256,8]{2,1,0:T(8,128)} copy(f32[12,256,8]{1,2,0:T(8,128)} %collective-permute-done.1) | data formatting | bytes 196608 | tf_op jit(solution)/shard_map/ppermute | solution.py:51
  58.5 1.1 pad_maximum_fusion.7
  59.6 4.0 %collective-permute-start.2 = (f32[12,8,144]{2,1,0:T(8,128)S(1)}, f32[12,8,144]{2,1,0:T(8,128)S(1)}, u32[]{:S(2)}, u32[]{:S(2)}) collective-permute-start(f32[12,8,144]{2,1,0:T(8,128)S(1)} %get-tuple-element.33), channel_id=1, source_target_pairs={{0,1},{1,2},{2,3},{3,4},{4,5},{5,6},{6,7},{7,0},{8,9},{9,10},{10,1... | collective-permute-start | bytes 165896 | tf_op jit(solution)/shard_map/ppermute | solution.py:49
  63.8 1.5 %collective-permute-done.2 = f32[12,8,144]{2,1,0:T(8,128)S(1)} collective-permute-done((f32[12,8,144]{2,1,0:T(8,128)S(1)}, f32[12,8,144]{2,1,0:T(8,128)S(1)}, u32[]{:S(2)}, u32[]{:S(2)}) %collective-permute-start.2) | collective-permute-done | bytes 55328 | tf_op jit(solution)/shard_map/ppermute | solution.py:49
  65.2 2.4 %collective-permute-done.3 = f32[12,8,144]{2,1,0:T(8,128)S(1)} collective-permute-done((f32[12,8,144]{2,1,0:T(8,128)S(1)}, f32[12,8,144]{2,1,0:T(8,128)S(1)}, u32[]{:S(2)}, u32[]{:S(2)}) %collective-permute-start.3) | collective-permute-done | bytes 55328 | tf_op jit(solution)/shard_map/ppermute | solution.py:51
  67.6 1.3 pad_maximum_fusion
  69.7 0.9 copy-done
  70.7 0.6 multiply_bitcast_fusion.5
  71.5 0.9 slice-done
  72.8 1.5 %copy-done.1 = f32[12,272,144]{2,1,0:T(8,128)S(1)} copy-done((f32[12,272,144]{2,1,0:T(8,128)S(1)}, f32[12,272,144]{2,1,0:T(8,128)}, u32[]{:S(2)}) %copy-start.1) | copy-done | bytes 1880088
  74.4 0.9 fusion.15
  75.3 0.9 fusion.19
  76.2 0.6 multiply_bitcast_fusion.2
  77.4 0.9 fusion.83
  78.3 0.9 fusion.71
  79.3 0.6 multiply_bitcast_fusion.11
  80.5 0.9 fusion.59
  81.4 1.1 fusion.48
  82.6 0.6 multiply_bitcast_fusion.8
  83.8 0.7 copy-done.4
  85.1 0.9 copy.41
  86.0 7.1 %all-to-all-start.2 = ((f32[2,256,128]{2,0,1:T(2,128)}), f32[2,256,128]{2,0,1:T(2,128)S(1)}, u32[]{:S(2)}, u32[]{:S(2)}) async-start(f32[2,256,128]{2,0,1:T(2,128)} %copy.41), calls=%async_computation.2 | async-start | bytes 524288 | tf_op jit(solution)/shard_map/all_to_all | solution.py:197
  93.2 0.6 dynamic-slice
  93.8 0.6 dynamic-slice.1
  95.7 0.6 dynamic-slice.2
  96.9 0.6 dynamic-slice.3
  98.4 1.2 fusion.98
  99.6 2.6 %maximum_dynamic-update-slice_fusion = f32[32]{0:T(128)S(1)} fusion(f32[32]{0:T(128)S(1)} %broadcast.160, u32[]{:T(128)} %bitcast.81, f32[1]{0:T(128)} %bitcast.80, f32[1]{0:T(128)} %bitcast.79, f32[1]{0:T(128)} %bitcast.78, f32[1]{0:T(128)} %bitcast.77), kind=kLoop, calls=%fused_computation.280 | loop fusion | flops 12 | bytes 148
  102.1 13.2 %all-reduce = f32[32]{0:T(128)S(1)} all-reduce(f32[32]{0:T(128)S(1)} %maximum_dynamic-update-slice_fusion), channel_id=2, replica_groups=mesh['gx_0'=8,'gx_1'=4,'gy_0'=4,'gy_1'=2] {'gx_0'}, use_global_device_ids=true, to_apply=%add | all-reduce | flops 32 | bytes 256
  115.7 8.4 %all-reduce.1 = f32[16]{0:T(128)S(1)} all-reduce(f32[16]{0:T(128)S(1)} %dynamic-update-slice.1), channel_id=3, replica_groups=mesh['gx_0'=8,'gx_1'=4,'gy_0'=4,'gy_1'=2] {'gx_1'}, use_global_device_ids=true, to_apply=%add.1 | all-reduce | flops 16 | bytes 128
  124.4 8.9 %all-reduce.2 = f32[16]{0:T(128)S(1)} all-reduce(f32[16]{0:T(128)S(1)} %dynamic-update-slice.2), channel_id=4, replica_groups=mesh['gx_0'=8,'gx_1'=4,'gy_0'=4,'gy_1'=2] {'gy_0'}, use_global_device_ids=true, to_apply=%add.2 | all-reduce | flops 16 | bytes 128
  133.6 9.1 %all-reduce.3 = f32[8]{0:T(128)S(1)} all-reduce(f32[8]{0:T(128)S(1)} %dynamic-update-slice.3), channel_id=5, replica_groups=mesh['gx_0'=8,'gx_1'=4,'gy_0'=4,'gy_1'=2] {'gy_1'}, use_global_device_ids=true, to_apply=%add.3 | all-reduce | flops 8 | bytes 64
  142.7 0.9 slice.886
  144.3 0.7 copy.51
  (83 shorter events, 7.3 us)
Async XLA Ops:
  0.6 11.5 %copy-start.8 = (f32[2,256,128]{2,1,0:T(8,128)S(1)}, f32[2,256,128]{2,1,0:T(8,128)}, u32[]{:S(2)}) copy-start(f32[2,256,128]{2,1,0:T(8,128)} %param.6) | copy-start | bytes 786436
  1.8 10.3 %copy-start.7 = (f32[3,256,128]{2,1,0:T(8,128)S(1)}, f32[3,256,128]{2,1,0:T(8,128)}, u32[]{:S(2)}) copy-start(f32[3,256,128]{2,1,0:T(8,128)} %param.7) | copy-start | bytes 1179652
  1.8 10.3 %copy-start.9 = (f32[256,128]{1,0:T(8,128)S(1)}, f32[256,128]{1,0:T(8,128)}, u32[]{:S(2)}) copy-start(f32[256,128]{1,0:T(8,128)} %param.9) | copy-start | bytes 393220
  2.9 9.3 %copy-start.10 = (f32[256,128]{1,0:T(8,128)S(1)}, f32[256,128]{1,0:T(8,128)}, u32[]{:S(2)}) copy-start(f32[256,128]{1,0:T(8,128)} %param.8) | copy-start | bytes 393220
  2.9 27.1 %all-to-all-start = ((f32[8,4,4,8,128]{4,3,1,2,0:T(8,128)}), f32[8,4,4,8,128]{4,3,1,2,0:T(8,128)S(1)}, u32[]{:S(2)}, u32[]{:S(2)}) async-start(f32[8,4,4,8,128]{4,3,1,2,0:T(8,128)} %copy.32), calls=%async_computation | async-start | bytes 1048576 | tf_op jit(solution)/shard_map/all_to_all | solution.py:33
  12.1 22.9 %copy-start.6 = (s32[256,128]{1,0:T(8,128)S(1)}, s32[256,128]{1,0:T(8,128)}, u32[]{:S(2)}) copy-start(s32[256,128]{1,0:T(8,128)} %param.10) | copy-start | bytes 393220
  30.9 12.8 %all-to-all-start.1 = ((f32[8,4,4,8,128]{4,3,0,2,1:T(8,128)}), f32[8,4,4,8,128]{4,3,0,2,1:T(8,128)S(1)}, u32[]{:S(2)}, u32[]{:S(2)}) async-start(f32[8,4,4,8,128]{4,3,0,2,1:T(8,128)} %copy.33), calls=%async_computation.1 | async-start | bytes 1048576 | tf_op jit(solution)/shard_map/all_to_all | solution.py:33
  43.7 0.8 copy-start.3
  48.1 6.8 %collective-permute-start = (f32[12,256,8]{1,2,0:T(8,128)S(1)}, f32[12,256,8]{1,2,0:T(8,128)S(1)}, u32[]{:S(2)}, u32[]{:S(2)}) collective-permute-start(f32[12,256,8]{1,2,0:T(8,128)S(1)} %copy.36), channel_id=1, source_target_pairs={{0,8},{8,16},{16,24},{24,32},{32,40},{40,48},{48,56},{56,64},{64,7... | collective-permute-start | bytes 294920 | tf_op jit(solution)/shard_map/ppermute | solution.py:49
  49.6 6.5 %collective-permute-start.1 = (f32[12,256,8]{1,2,0:T(8,128)}, f32[12,256,8]{1,2,0:T(8,128)}, u32[]{:S(2)}, u32[]{:S(2)}) collective-permute-start(f32[12,256,8]{1,2,0:T(8,128)} %copy.37), channel_id=1, source_target_pairs={{8,0},{16,8},{24,16},{32,24},{40,32},{48,40},{56,48},{64,56},{72,6... | collective-permute-start | bytes 294920 | tf_op jit(solution)/shard_map/ppermute | solution.py:51
  58.5 9.1 %copy-start.2 = (f32[12,256,8]{2,1,0:T(8,128)S(1)}, f32[12,256,8]{2,1,0:T(8,128)}, u32[]{:S(2)}) copy-start(f32[12,256,8]{2,1,0:T(8,128)} %copy.39) | copy-start | bytes 294916
  59.6 5.6 %collective-permute-start.2 = (f32[12,8,144]{2,1,0:T(8,128)S(1)}, f32[12,8,144]{2,1,0:T(8,128)S(1)}, u32[]{:S(2)}, u32[]{:S(2)}) collective-permute-start(f32[12,8,144]{2,1,0:T(8,128)S(1)} %get-tuple-element.33), channel_id=1, source_target_pairs={{0,1},{1,2},{2,3},{3,4},{4,5},{5,6},{6,7},{7,0},{8,9},{9,10},{10,1... | collective-permute-start | bytes 165896 | tf_op jit(solution)/shard_map/ppermute | solution.py:49
  63.6 4.0 %collective-permute-start.3 = (f32[12,8,144]{2,1,0:T(8,128)S(1)}, f32[12,8,144]{2,1,0:T(8,128)S(1)}, u32[]{:S(2)}, u32[]{:S(2)}) collective-permute-start(f32[12,8,144]{2,1,0:T(8,128)S(1)} %get-tuple-element.34), channel_id=1, source_target_pairs={{1,0},{2,1},{3,2},{4,3},{5,4},{6,5},{7,6},{0,7},{9,8},{10,9},{11,1... | collective-permute-start | bytes 165896 | tf_op jit(solution)/shard_map/ppermute | solution.py:51
  68.9 1.7 %copy-start = (f32[12,272,144]{2,1,0:T(8,128)}, f32[12,272,144]{2,1,0:T(8,128)S(1)}, u32[]{:S(2)}) copy-start(f32[12,272,144]{2,1,0:T(8,128)S(1)} %pad_maximum_fusion) | copy-start | bytes 5640196
  71.3 1.2 slice-start
  72.4 1.9 %copy-start.1 = (f32[12,272,144]{2,1,0:T(8,128)S(1)}, f32[12,272,144]{2,1,0:T(8,128)}, u32[]{:S(2)}) copy-start(f32[12,272,144]{2,1,0:T(8,128)} %copy-done) | copy-start | bytes 5640196
  83.4 1.0 copy-start.4
  85.0 8.2 %copy-start.14 = (u32[256]{0:T(256)S(1)}, u32[256]{0:T(256)}, u32[]{:S(2)}) copy-start(u32[256]{0:T(256)} %constant.17) | copy-start | bytes 3076
  85.0 8.7 %copy-start.13 = (u32[256]{0:T(256)S(1)}, u32[256]{0:T(256)}, u32[]{:S(2)}) copy-start(u32[256]{0:T(256)} %constant.40) | copy-start | bytes 3076
  85.0 10.6 %copy-start.12 = (u32[256]{0:T(256)S(1)}, u32[256]{0:T(256)}, u32[]{:S(2)}) copy-start(u32[256]{0:T(256)} %constant.45) | copy-start | bytes 3076
  85.0 11.9 %copy-start.11 = (u32[256]{0:T(256)S(1)}, u32[256]{0:T(256)}, u32[]{:S(2)}) copy-start(u32[256]{0:T(256)} %constant.50) | copy-start | bytes 3076
  85.1 14.4 %copy-start.5 = (f32[2,256,128]{2,1,0:T(8,128)}, f32[2,256,128]{2,1,0:T(8,128)S(1)}, u32[]{:S(2)}) copy-start(f32[2,256,128]{2,1,0:T(8,128)S(1)} %get-tuple-element.13) | copy-start | bytes 786436
  86.0 58.2 %all-to-all-start.2 = ((f32[2,256,128]{2,0,1:T(2,128)}), f32[2,256,128]{2,0,1:T(2,128)S(1)}, u32[]{:S(2)}, u32[]{:S(2)}) async-start(f32[2,256,128]{2,0,1:T(2,128)} %copy.41), calls=%async_computation.2 | async-start | bytes 524288 | tf_op jit(solution)/shard_map/all_to_all | solution.py:197
